TPU v7x, 32 devices: a whole 2x2x4 slice. The times are simulated.
32 devices in a mesh: gz: 16 (over z, x, core), xy: 2 (over y).
Axes of the slice: x: 2, y: 2, z: 4, core: 2. Of those that a mesh axis runs over, the one named last changes fastest.
Arguments:
- coords: float32 [3, 32, 4, 128], P(None, 'gz', 'xy'), may hold values from 0 to 1
- species: int32 [32, 4, 128], P('gz', 'xy'), may hold values from 0 to 7
- centers: int32 [32, 4, 128], P('gz', 'xy'), may hold values from 0 to 127
- others: int32 [32, 4, 128], P('gz', 'xy'), may hold values from 0 to 1151
- live_count: int32 [32, 4], P('gz', 'xy'), may hold values from 42 to 128
- in_weight: float32 [24, 128], replicated, may hold values from -1.25 to 1.25
- env_weight: float32 [128, 32], replicated, may hold values from -0.5 to 0.5
- up_weight: float32 [160, 128], replicated, may hold values from -0.5 to 0.5
- out_weight: float32 [128], replicated, may hold values from -0.5 to 0.5
Outputs:
- atom_energy: float32 [32, 4, 128], P('gz', 'xy')
- forces: float32 [3, 32, 4, 128], P(None, 'gz', 'xy')
Inputs may be any that keep to these rules, and one draw needn't show every extreme that they name: Edge slots at or after live_count of a bin are padding; at most 128 are live.
All inputs are finite; a program needn't handle non-finite values.
Results may differ from a plain program's by a relative error of at most 0.0018.
Values may be sent and summed in bfloat16 or wider, within the bound.
A program may use at most 64 MiB of HBM per device.

v0:
```python
import jax
import jax.numpy as jnp
from jax import lax
from jax.sharding import PartitionSpec as P

NB = 8
SPEC = 8


SOFTEN = 0.01
CUTOFF = 3.5
HIGH = lax.Precision.HIGHEST


def extended_2(block, sides, width):
    for axis, dim in sides:
        count = lax.axis_size(axis)
        forward = [(i, i + 1) for i in range(count - 1)]
        forward.append((count - 1, 0))
        backward = [(target, source) for source, target in forward]
        low = lax.ppermute(
            lax.slice_in_dim(block, block.shape[dim] - width, None, axis=dim), axis, forward
        )
        high = lax.ppermute(lax.slice_in_dim(block, 0, width, axis=dim), axis, backward)
        block = jnp.concatenate([low, block, high], axis=dim)
    return block


def atom_table(indices):
    return (indices[..., None] == jnp.arange(128)).astype(jnp.float32)


def pick_center(lattice, center_hot):
    return jnp.einsum("fabn,aben->fabe", lattice, center_hot, precision=HIGH)


def pick_other(lattice_ext, others):
    depth_bins = lattice_ext.shape[-3] - 2
    span_bins = lattice_ext.shape[-2] - 2
    other_hot = atom_table(others % 128)
    placement = others // 128
    gathered = jnp.zeros((lattice_ext.shape[0],) + others.shape, jnp.float32)
    for offset in range(9):
        start_z = offset // 3
        start_x = offset % 3
        block = lattice_ext[:, start_z : start_z + depth_bins, start_x : start_x + span_bins, :]
        chosen = (placement == offset).astype(jnp.float32)[None]
        gathered = (
            gathered + jnp.einsum("fabn,aben->fabe", block, other_hot, precision=HIGH) * chosen
        )
    return gathered


def live_mask(live_count, edge_count):
    return (jnp.arange(edge_count)[None, None, :] < live_count[..., None]).astype(jnp.float32)


def geometry(coord_ext, spec_ext, centers, others, in_weight):
    center_hot = atom_table(centers)
    at_center = pick_center(coord_ext[:, 1:-1, 1:-1], center_hot)
    at_other = pick_other(coord_ext, others)
    placement = others // 128
    shift_z = (placement // 3 - 1).astype(jnp.float32)
    shift_x = (placement % 3 - 1).astype(jnp.float32)
    along_z = shift_z + at_other[0] - at_center[0]
    across = shift_x + at_other[1] - at_center[1]
    along_y = at_other[2] - at_center[2]
    distance = jnp.sqrt(along_z * along_z + across * across + along_y * along_y + SOFTEN)
    scaled = distance / CUTOFF
    envelope = (1.0 - scaled * scaled) ** 2
    orders = jnp.arange(1, NB + 1).astype(jnp.float32)[:, None, None, None]
    radial = jnp.sin(orders * jnp.pi * scaled[None]) / distance[None] * envelope[None]
    species_ids = jnp.arange(SPEC)[:, None, None, None]
    spec_table = (spec_ext[None] == species_ids).astype(jnp.float32)
    spec_center = pick_center(spec_table[:, 1:-1, 1:-1], center_hot)
    spec_other = pick_other(spec_table, others)
    inputs = jnp.concatenate([radial, spec_center, spec_other], axis=0)
    latent = jax.nn.silu(jnp.einsum("kabe,kl->labe", inputs, in_weight, precision=HIGH))
    harmonics = jnp.stack(
        [jnp.ones_like(distance), along_z / distance, across / distance, along_y / distance]
    )
    return (latent, harmonics, envelope)


def features(latent, harmonics, centers, live_count, env_weight):
    edge_count = centers.shape[-1]
    weights = (
        jnp.einsum("labe,lc->cabe", latent, env_weight, precision=HIGH)
        * live_mask(live_count, edge_count)[None]
    )
    messages = (weights[:, None] * harmonics[None]).reshape((-1,) + centers.shape)
    one_hot = atom_table(centers)
    return jnp.einsum("fabe,aben->fabn", messages, one_hot, precision=HIGH) * (128.0 / edge_count)


def energy(latent, envelope, feature_ext, centers, others, live_count, up_weight, out_weight):
    channels = feature_ext.shape[0] // 4
    one_hot = atom_table(centers)
    feat_center = pick_center(feature_ext[:, 1:-1, 1:-1], one_hot)
    feat_other = pick_other(feature_ext, others)
    products = (feat_center * feat_other).reshape((channels, 4) + centers.shape).sum(axis=1)
    joined = jnp.concatenate([latent, products], axis=0)
    hidden = jax.nn.silu(jnp.einsum("kabe,kl->labe", joined, up_weight, precision=HIGH))
    edge_energy = (
        jnp.einsum("labe,l->abe", hidden, out_weight, precision=HIGH)
        * envelope
        * live_mask(live_count, centers.shape[-1])
    )
    atom_energy = jnp.einsum("abe,aben->abn", edge_energy, one_hot, precision=HIGH)
    return (jnp.sum(edge_energy), atom_energy)


def fold_wide(ghost, depth):
    padded = extended_2(ghost, (("gz", 1), ("xy", 2)), depth)
    rows_z = ghost.shape[1] - 2 * depth
    rows_x = ghost.shape[2] - 2 * depth
    parts_z = [
        (slice(0, depth), slice(0, depth)),
        (slice(2 * depth, 2 * depth + rows_z), slice(0, rows_z)),
        (slice(rows_z + 3 * depth, rows_z + 4 * depth), slice(rows_z - depth, rows_z)),
    ]
    parts_x = [
        (slice(0, depth), slice(0, depth)),
        (slice(2 * depth, 2 * depth + rows_x), slice(0, rows_x)),
        (slice(rows_x + 3 * depth, rows_x + 4 * depth), slice(rows_x - depth, rows_x)),
    ]
    result = jnp.zeros((ghost.shape[0], rows_z, rows_x, ghost.shape[3]), jnp.float32)
    for source_z, target_z in parts_z:
        for source_x, target_x in parts_x:
            result = result.at[:, target_z, target_x].add(padded[:, source_z, source_x])
    return result


def body(
    coords, species, centers, others, live_count, in_weight, env_weight, up_weight, out_weight
):
    packed = jnp.concatenate([coords, species.astype(jnp.float32)[None]], axis=0)
    extended = extended_2(packed, (("gz", 1), ("xy", 2)), 2)
    spec_wide = extended[3].astype(jnp.int32)
    coord_wide = extended[:3]
    edge_count = centers.shape[-1]
    lists = jnp.concatenate([centers, others, live_count[..., None]], axis=-1)
    lists_ext = extended_2(lists, (("gz", 0), ("xy", 1)), 1)
    centers_ext = lists_ext[..., :edge_count]
    others_ext = lists_ext[..., edge_count : 2 * edge_count]
    live_ext = lists_ext[..., 2 * edge_count]

    def whole_energy(coord_now):
        latent, harmonics, envelope = geometry(
            coord_now, spec_wide, centers_ext, others_ext, in_weight
        )
        feat = features(latent, harmonics, centers_ext, live_ext, env_weight)
        rounded = lax.optimization_barrier(feat.astype(jnp.bfloat16)).astype(jnp.float32)
        through = feat + lax.stop_gradient(rounded - feat)
        return energy(
            latent[:, 1:-1, 1:-1],
            envelope[1:-1, 1:-1],
            through,
            centers,
            others,
            live_count,
            up_weight,
            out_weight,
        )

    (energy_sum, atom_energy), coord_grad = jax.value_and_grad(whole_energy, has_aux=True)(
        coord_wide
    )
    forces = -fold_wide(coord_grad, 2)
    return (atom_energy, forces)


def solution(mesh):
    in_specs = (
        P(None, "gz", "xy", None),
        P("gz", "xy", None),
        P("gz", "xy", None),
        P("gz", "xy", None),
        P("gz", "xy"),
        P(),
        P(),
        P(),
        P(),
    )
    out_specs = (P("gz", "xy", None), P(None, "gz", "xy", None))
    return jax.shard_map(body, mesh=mesh, in_specs=in_specs, out_specs=out_specs, check_vma=False)
```

profile of v0, /device:TPU:0, one launch (start us, length us, event | category | flops | bytes accessed | tf_op | source)
XLA Modules:
  0.0 82.1 jit_solution(4140950537204731720)
XLA Ops:
  0.6 0.7 convert_element_type.108
  1.4 0.7 copy.74
  2.1 5.5 %collective-permute-start.5 = (f32[4,2,2,128]{3,0,2,1:T(4,128)S(1)}, f32[4,2,2,128]{3,0,2,1:T(4,128)S(1)}, u32[]{:S(2)}, u32[]{:S(2)}) collective-permute-start(f32[4,2,2,128]{3,0,2,1:T(4,128)S(1)} %pad_maximum_fusion.7), channel_id=1, source_target_pairs={{2,0},{4,2},{6,4},{8,6},{10,8},{12,10},{14,12},{16,14},{18,16},{20... | collective-permute-start | bytes 24584 | tf_op jit(solution)/shard_map/ppermute | solution.py:24
  7.8 4.5 %collective-permute-start.1 = (s32[1,2,257]{2,1,0:T(2,128)S(1)}, s32[1,2,257]{2,1,0:T(2,128)S(1)}, u32[]{:S(2)}, u32[]{:S(2)}) collective-permute-start(s32[1,2,257]{2,1,0:T(2,128)S(1)} %get-tuple-element.250), channel_id=1, source_target_pairs={{2,0},{4,2},{6,4},{8,6},{10,8},{12,10},{14,12},{16,14},{18,16},{20... | collective-permute-start | bytes 6176 | tf_op jit(solution)/shard_map/ppermute | solution.py:24
  12.3 1.2 %collective-permute-done = s32[1,2,257]{2,1,0:T(2,128)S(1)} collective-permute-done((s32[1,2,257]{2,1,0:T(2,128)S(1)}, s32[1,2,257]{2,1,0:T(2,128)S(1)}, u32[]{:S(2)}, u32[]{:S(2)}) %collective-permute-start) | collective-permute-done | bytes 2088 | tf_op jit(solution)/shard_map/ppermute | solution.py:21
  13.6 1.6 %collective-permute-start.2 = (s32[4,1,257]{2,1,0:T(1,128)S(1)}, s32[4,1,257]{2,1,0:T(1,128)S(1)}, u32[]{:S(2)}, u32[]{:S(2)}) collective-permute-start(s32[4,1,257]{2,1,0:T(1,128)S(1)} %get-tuple-element.232), channel_id=1, source_target_pairs={{0,1},{1,0},{2,3},{3,2},{4,5},{5,4},{6,7},{7,6},{8,9},{9,8},{10,11... | collective-permute-start | bytes 12344 | tf_op jit(solution)/shard_map/ppermute | solution.py:21
  15.2 0.5 collective-permute-start.3
  15.7 1.6 %collective-permute-done.2 = s32[4,1,257]{2,1,0:T(1,128)S(1)} collective-permute-done((s32[4,1,257]{2,1,0:T(1,128)S(1)}, s32[4,1,257]{2,1,0:T(1,128)S(1)}, u32[]{:S(2)}, u32[]{:S(2)}) %collective-permute-start.2) | collective-permute-done | bytes 4144 | tf_op jit(solution)/shard_map/ppermute | solution.py:21
  17.3 1.5 %collective-permute-done.3 = s32[4,1,257]{2,1,0:T(1,128)S(1)} collective-permute-done((s32[4,1,257]{2,1,0:T(1,128)S(1)}, s32[4,1,257]{2,1,0:T(1,128)S(1)}, u32[]{:S(2)}, u32[]{:S(2)}) %collective-permute-start.3) | collective-permute-done | bytes 4144 | tf_op jit(solution)/shard_map/ppermute | solution.py:24
  19.1 0.6 collective-permute-start.7
  19.7 1.5 %collective-permute-start.6 = (f32[4,6,2,128]{3,0,2,1:T(4,128)S(1)}, f32[4,6,2,128]{3,0,2,1:T(4,128)S(1)}, u32[]{:S(2)}, u32[]{:S(2)}) collective-permute-start(f32[4,6,2,128]{3,0,2,1:T(4,128)S(1)} %pad_maximum_fusion.6), channel_id=1, source_target_pairs={{0,1},{1,0},{2,3},{3,2},{4,5},{5,4},{6,7},{7,6},{8,9},{9,8},{10,11... | collective-permute-start | bytes 73736 | tf_op jit(solution)/shard_map/ppermute | solution.py:21
  21.3 1.7 %collective-permute-done.7 = f32[4,6,2,128]{3,0,2,1:T(4,128)S(1)} collective-permute-done((f32[4,6,2,128]{3,0,2,1:T(4,128)S(1)}, f32[4,6,2,128]{3,0,2,1:T(4,128)S(1)}, u32[]{:S(2)}, u32[]{:S(2)}) %collective-permute-start.7) | collective-permute-done | bytes 24608 | tf_op jit(solution)/shard_map/ppermute | solution.py:24
  23.0 0.5 collective-permute-done.6
  23.6 1.0 %fusion.57 = f32[4,4,128,3]{2,3,1,0:T(4,128)S(1)} fusion(s32[4,4,128]{2,1,0:T(4,128)S(1)} %get-tuple-element.231, f32[4,6,6,128]{3,0,2,1:T(4,128)S(1)} %pad_maximum_fusion), kind=kOutput, calls=%fused_computation.118 | convolution fusion | flops 9699328 | bytes 65536 | tf_op jit(solution)/shard_map/jvp(fabn,aben->fabe)/dot_general | solution.py:34
  24.6 1.0 %convolution_multiply_fusion.26 = f32[4,4,128,3]{2,3,1,0:T(4,128)S(1)} fusion(s32[4,4,128]{2,1,0:T(4,128)S(1)} %get-tuple-element.230, f32[4,6,6,128]{3,0,2,1:T(4,128)S(1)} %pad_maximum_fusion, f32[4,4,128]{2,1,0:T(4,128)S(1)} %get-tuple-element.246), kind=kOutput, calls=%fused_computation.84 | convolution fusion | flops 9705472 | bytes 73728 | tf_op jit(solution)/shard_map/jvp(fabn,aben->fabe)/dot_general | solution.py:49
  25.6 0.7 convolution_multiply_fusion.17
  26.3 0.6 convolution_bitcast_fusion.17
  26.9 0.7 convolution_multiply_fusion.15
  27.6 0.6 convolution_multiply_fusion.16
  28.3 1.0 %fusion.28 = f32[4,4,128,3]{2,3,1,0:T(4,128)S(1)} fusion(f32[4,4,128,3]{2,3,1,0:T(4,128)S(1)} %convolution_multiply_fusion.26, s32[4,4,128]{2,1,0:T(4,128)S(1)} %get-tuple-element.230, f32[4,6,4,128]{3,0,2,1:T(4,128)S(1)} %get-tuple-element.221, f32[4,4,128]{2,1,0:T(4,128)S(1)} %get-tuple-element.247), kind=kOutput, calls=%fused_computation.86 | convolution fusion | flops 9711616 | bytes 106496 | tf_op jit(solution)/shard_map/jvp(fabn,aben->fabe)/dot_general | solution.py:49
  29.2 1.0 %fusion.27 = f32[4,4,128,3]{2,3,1,0:T(4,128)S(1)} fusion(f32[4,4,128,3]{2,3,1,0:T(4,128)S(1)} %fusion.28, s32[4,4,128]{2,1,0:T(4,128)S(1)} %get-tuple-element.230, f32[4,6,4,128]{3,0,2,1:T(4,128)S(1)} %get-tuple-element.220, f32[4,4,128]{2,1,0:T(4,128)S(1)} %get-tuple-element.245), kind=kOutput, calls=%fused_computation.83 | convolution fusion | flops 9711616 | bytes 106496 | tf_op jit(solution)/shard_map/jvp(fabn,aben->fabe)/dot_general | solution.py:49
  30.3 1.0 %fusion.26 = f32[4,4,128,3]{2,3,1,0:T(4,128)S(1)} fusion(f32[4,4,128,3]{2,3,1,0:T(4,128)S(1)} %fusion.27, s32[4,4,128]{2,1,0:T(4,128)S(1)} %get-tuple-element.230, f32[4,6,4,128]{3,0,2,1:T(4,128)S(1)} %get-tuple-element.221, f32[4,4,128]{2,1,0:T(4,128)S(1)} %get-tuple-element.244), kind=kOutput, calls=%fused_computation.81 | convolution fusion | flops 9711616 | bytes 106496 | tf_op jit(solution)/shard_map/jvp(fabn,aben->fabe)/dot_general | solution.py:49
  31.3 0.7 convolution_multiply_fusion.14
  31.9 1.0 %fusion.25 = f32[4,4,128,3]{2,3,1,0:T(4,128)S(1)} fusion(f32[4,4,128,3]{2,3,1,0:T(4,128)S(1)} %fusion.26, s32[4,4,128]{2,1,0:T(4,128)S(1)} %get-tuple-element.230, f32[4,6,6,128]{3,0,2,1:T(4,128)S(1)} %pad_maximum_fusion, f32[4,4,128]{2,1,0:T(4,128)S(1)} %get-tuple-element.243), kind=kOutput, calls=%fused_computation.79 | convolution fusion | flops 9711616 | bytes 106496 | tf_op jit(solution)/shard_map/jvp(fabn,aben->fabe)/dot_general | solution.py:49
  32.9 0.7 convolution_multiply_fusion.12
  33.6 1.0 %fusion.24 = f32[4,4,128,3]{2,3,1,0:T(4,128)S(1)} fusion(f32[4,4,128,3]{2,3,1,0:T(4,128)S(1)} %fusion.25, s32[4,4,128]{2,1,0:T(4,128)S(1)} %get-tuple-element.230, f32[4,6,4,128]{3,0,2,1:T(4,128)S(1)} %get-tuple-element.220, f32[4,4,128]{2,1,0:T(4,128)S(1)} %get-tuple-element.242), kind=kOutput, calls=%fused_computation.77 | convolution fusion | flops 9711616 | bytes 106496 | tf_op jit(solution)/shard_map/jvp(fabn,aben->fabe)/dot_general | solution.py:49
  34.6 1.0 %fusion.23 = f32[4,4,128,3]{2,3,1,0:T(4,128)S(1)} fusion(f32[4,4,128,3]{2,3,1,0:T(4,128)S(1)} %fusion.24, s32[4,4,128]{2,1,0:T(4,128)S(1)} %get-tuple-element.230, f32[4,6,4,128]{3,0,2,1:T(4,128)S(1)} %get-tuple-element.221, f32[4,4,128]{2,1,0:T(4,128)S(1)} %get-tuple-element.248), kind=kOutput, calls=%fused_computation.75 | convolution fusion | flops 9711616 | bytes 106496 | tf_op jit(solution)/shard_map/jvp(fabn,aben->fabe)/dot_general | solution.py:49
  35.6 0.7 convolution_multiply_fusion.11
  36.2 1.0 %fusion.22 = f32[4,4,128,3]{2,3,1,0:T(4,128)S(1)} fusion(f32[4,4,128,3]{2,3,1,0:T(4,128)S(1)} %fusion.23, s32[4,4,128]{2,1,0:T(4,128)S(1)} %get-tuple-element.230, f32[4,6,6,128]{3,0,2,1:T(4,128)S(1)} %pad_maximum_fusion, f32[4,4,128]{2,1,0:T(4,128)S(1)} %get-tuple-element.241), kind=kOutput, calls=%fused_computation.73 | convolution fusion | flops 9711616 | bytes 106496 | tf_op jit(solution)/shard_map/jvp(fabn,aben->fabe)/dot_general | solution.py:49
  37.2 0.7 convolution_multiply_fusion.10
  37.9 1.0 %fusion.21 = f32[3,4,4,128]{3,0,2,1:T(4,128)S(1)} fusion(f32[4,4,128,3]{2,3,1,0:T(4,128)S(1)} %fusion.22, s32[4,4,128]{2,1,0:T(4,128)S(1)} %get-tuple-element.230, f32[4,6,4,128]{3,0,2,1:T(4,128)S(1)} %get-tuple-element.220, f32[4,4,128]{2,1,0:T(4,128)S(1)} %get-tuple-element.206), kind=kOutput, calls=%fused_computation.71 | convolution fusion | flops 9711616 | bytes 106496 | tf_op jit(solution)/shard_map/jvp(fabn,aben->fabe)/dot_general | solution.py:49
  39.4 0.7 fusion.14
  40.1 0.7 fusion.19
  40.8 1.2 %fusion.55 = (f32[128,4,4,128]{3,0,2,1:T(8,128)S(1)}, f32[128,4,4,128]{3,0,2,1:T(8,128)S(1)}) fusion(f32[24,128]{1,0:T(8,128)S(1)} %copy-done.6, f32[8,4,4,128]{3,0,2,1:T(8,128)S(1)} %fusion.19, f32[8,4,4,128]{3,0,2,1:T(8,128)S(1)} %convolution_bitcast_fusion.17, f32[8,4,4,128]{3,0,2,1:T(8,128)S(1)} %fusion.189), kind=kOutput, calls=%fused_computation.115 | convolution fusion | flops 76644352 | bytes 2306048 | tf_op jit(solution)/shard_map/jvp(kabe,kl->labe)/dot_general | solution.py:78
  42.0 0.7 copy-done.2
  42.7 0.7 fusion.10
  43.6 2.0 %fusion.244 = (bf16[128,4,4,128]{0,3,2,1:T(8,128)(2,1)S(1)}, f32[128,4,4,128]{0,3,2,1:T(8,128)S(1)}) fusion(f32[128,4,4,128]{3,0,2,1:T(8,128)S(1)} %bitcast.240, s32[4,4,128]{2,1,0:T(4,128)S(1)} %get-tuple-element.231), kind=kOutput, calls=%fused_computation.413 | convolution fusion | flops 403439616 | bytes 2629632 | tf_op jit(solution)/shard_map/jvp(fabe,aben->fabn)/dot_general | solution.py:93
  47.2 0.5 fusion.7
  49.6 0.5 fusion.2
  50.7 1.1 %convolution_bitcast_fusion.4 = f32[128,2,2,128]{0,3,2,1:T(8,128)S(1)} fusion(f32[32,2,2,128]{3,0,2,1:T(8,128)S(1)} %reduce_sum.51, f32[128,2,2,128]{3,0,2,1:T(8,128)S(1)} %slice.492, f32[160,128]{1,0:T(8,128)S(1)} %copy-done), kind=kOutput, calls=%fused_computation.7 | convolution fusion | flops 125911040 | bytes 671744 | tf_op jit(solution)/shard_map/jvp(kabe,kl->labe)/dot_general | solution.py:103
  52.3 0.6 convolution_bitcast_fusion.3
  52.9 0.7 copy-done.1
  57.5 1.3 %fusion.32 = f32[4,4,128,128]{3,2,1,0:T(8,128)S(1)} fusion(f32[128,2,2,128]{3,0,2,1:T(8,128)S(1)} %convolution_bitcast_fusion.5, f32[128,2,2,128]{3,0,2,1:T(8,128)S(1)} %convolution_bitcast_fusion.6, f32[128,2,2,128]{3,0,2,1:T(8,128)S(1)} %convolution_bitcast_fusion.7, f32[128,2,2,128]{3,0,2,1:T(8,128)S(1)} %convolution_bitcast_fusion.8, ...), kind=kOutput, calls=%fused_computation.89 | convolution fusion | flops 405274624 | bytes 3678208 | tf_op jit(solution)/shard_map/transpose(jvp(fabe,aben->fabn))/dot_general | solution.py:93
  58.8 0.9 %multiply_reduce_fusion.1 = (f32[4,4,4,128]{3,0,2,1:T(4,128)S(1)}, f32[32,4,4,128]{3,0,2,1:T(8,128)S(1)}) fusion(f32[32,4,4,4,128]{4,1,0,3,2:T(4,128)S(1)} %bitcast.243, f32[32,4,4,128]{3,0,2,1:T(8,128)S(1)} %fusion.10, f32[4,4,4,128]{3,0,2,1:T(4,128)S(1)} %copy.79), kind=kLoop, calls=%fused_computation.94 | loop fusion | flops 974848 | bytes 1638400 | tf_op jit(solution)/shard_map/transpose(jvp())/reduce_sum | solution.py:91
  59.7 1.0 %fusion = f32[128,4,4,128]{3,0,2,1:T(8,128)S(1)} fusion(f32[128,2,2,128]{3,0,2,1:T(8,128)S(1)} %slice-done, f32[32,4,4,128]{3,0,2,1:T(8,128)S(1)} %get-tuple-element.189, f32[4,4,128]{2,1,0:T(4,128)S(1)} %fusion.227, f32[128,32]{0,1:T(8,128)S(1)} %copy-done.2), kind=kOutput, calls=%fused_computation.4 | convolution fusion | flops 100990976 | bytes 1597440 | tf_op jit(solution)/shard_map/transpose(jvp(labe,lc->cabe))/dot_general | solution.py:88
  60.8 1.2 %convolution_bitcast_fusion.16 = f32[24,4,4,128]{3,0,2,1:T(8,128)S(1)} fusion(f32[128,4,4,128]{3,0,2,1:T(8,128)S(1)} %get-tuple-element.261, f32[128,4,4,128]{3,0,2,1:T(8,128)S(1)} %fusion, f32[24,128]{1,0:T(8,128)S(1)} %copy-done.6), kind=kOutput, calls=%fused_computation.39 | convolution fusion | flops 77856768 | bytes 2306048 | tf_op jit(solution)/shard_map/transpose(jvp(kabe,kl->labe))/dot_general | solution.py:78
  62.5 0.7 convolution_bitcast_fusion.18
  63.3 0.7 convolution_bitcast_fusion.19
  64.0 0.7 convolution_bitcast_fusion.23
  64.7 0.7 convolution_bitcast_fusion.22
  65.4 0.7 convolution_bitcast_fusion.21
  66.2 0.7 convolution_bitcast_fusion.20
  66.9 0.7 convolution_bitcast_fusion.27
  67.6 0.7 convolution_bitcast_fusion.26
  68.3 0.7 convolution_bitcast_fusion.25
  69.1 0.7 convolution_bitcast_fusion.24
  69.9 4.4 %collective-permute-start.9 = (f32[3,2,6,128]{3,0,2,1:T(4,128)S(1)}, f32[3,2,6,128]{3,0,2,1:T(4,128)S(1)}, u32[]{:S(2)}, u32[]{:S(2)}) collective-permute-start(f32[3,2,6,128]{3,0,2,1:T(4,128)S(1)} %get-tuple-element.212), channel_id=1, source_target_pairs={{2,0},{4,2},{6,4},{8,6},{10,8},{12,10},{14,12},{16,14},{18,16},{20... | collective-permute-start | bytes 55304 | tf_op jit(solution)/shard_map/ppermute | solution.py:24
  74.4 1.5 %collective-permute-done.8 = f32[3,2,6,128]{3,0,2,1:T(4,128)S(1)} collective-permute-done((f32[3,2,6,128]{3,0,2,1:T(4,128)S(1)}, f32[3,2,6,128]{3,0,2,1:T(4,128)S(1)}, u32[]{:S(2)}, u32[]{:S(2)}) %collective-permute-start.8) | collective-permute-done | bytes 18464 | tf_op jit(solution)/shard_map/ppermute | solution.py:21
  75.9 1.6 %collective-permute-start.10 = (f32[3,10,2,128]{3,0,2,1:T(4,128)S(1)}, f32[3,10,2,128]{3,0,2,1:T(4,128)S(1)}, u32[]{:S(2)}, u32[]{:S(2)}) collective-permute-start(f32[3,10,2,128]{3,0,2,1:T(4,128)S(1)} %get-tuple-element.209), channel_id=1, source_target_pairs={{0,1},{1,0},{2,3},{3,2},{4,5},{5,4},{6,7},{7,6},{8,9},{9,8},{10,11... | collective-permute-start | bytes 92168 | tf_op jit(solution)/shard_map/ppermute | solution.py:21
  77.5 0.5 collective-permute-start.11
  78.0 0.9 %fusion.130 = f32[2,2,1,128]{3,2,1,0:T(1,128)} fusion(f32[2,2,128,1]{2,3,1,0:T(1,128)S(1)} %bitcast.269, s32[2,2,128]{2,1,0:T(2,128)S(1)} %copy-done.3), kind=kOutput, calls=%fused_computation.197 | convolution fusion | flops 851968 | bytes 6144 | tf_op jit(solution)/shard_map/jvp(abe,aben->abn)/dot_general | solution.py:109
  78.9 1.1 %collective-permute-done.10 = f32[3,10,2,128]{3,0,2,1:T(4,128)S(1)} collective-permute-done((f32[3,10,2,128]{3,0,2,1:T(4,128)S(1)}, f32[3,10,2,128]{3,0,2,1:T(4,128)S(1)}, u32[]{:S(2)}, u32[]{:S(2)}) %collective-permute-start.10) | collective-permute-done | bytes 30752 | tf_op jit(solution)/shard_map/ppermute | solution.py:21
  80.0 1.5 %collective-permute-done.11 = f32[3,10,2,128]{3,0,2,1:T(4,128)S(1)} collective-permute-done((f32[3,10,2,128]{3,0,2,1:T(4,128)S(1)}, f32[3,10,2,128]{3,0,2,1:T(4,128)S(1)}, u32[]{:S(2)}, u32[]{:S(2)}) %collective-permute-start.11) | collective-permute-done | bytes 30752 | tf_op jit(solution)/shard_map/ppermute | solution.py:24
  81.5 0.6 copy.106
  (93 shorter events, 10.6 us)
Async XLA Ops:
  0.6 50.1 %copy-start = (f32[160,128]{1,0:T(8,128)S(1)}, f32[160,128]{1,0:T(8,128)}, u32[]{:S(2)}) copy-start(f32[160,128]{1,0:T(8,128)} %param.52) | copy-start | bytes 245764
  2.1 5.5 %copy-start.5 = (s32[2,2]{1,0:T(2,128)S(1)}, s32[2,2]{1,0:T(2,128)}, u32[]{:S(2)}) copy-start(s32[2,2]{1,0:T(2,128)} %param.49) | copy-start | bytes 52
  2.1 5.6 %copy-start.3 = (s32[2,2,128]{2,1,0:T(2,128)S(1)}, s32[2,2,128]{2,1,0:T(2,128)}, u32[]{:S(2)}) copy-start(s32[2,2,128]{2,1,0:T(2,128)} %param.47) | copy-start | bytes 6148
  2.1 5.6 %copy-start.4 = (s32[2,2,128]{2,1,0:T(2,128)S(1)}, s32[2,2,128]{2,1,0:T(2,128)}, u32[]{:S(2)}) copy-start(s32[2,2,128]{2,1,0:T(2,128)} %param.48) | copy-start | bytes 6148
  2.1 17.0 %collective-permute-start.5 = (f32[4,2,2,128]{3,0,2,1:T(4,128)S(1)}, f32[4,2,2,128]{3,0,2,1:T(4,128)S(1)}, u32[]{:S(2)}, u32[]{:S(2)}) collective-permute-start(f32[4,2,2,128]{3,0,2,1:T(4,128)S(1)} %pad_maximum_fusion.7), channel_id=1, source_target_pairs={{2,0},{4,2},{6,4},{8,6},{10,8},{12,10},{14,12},{16,14},{18,16},{20... | collective-permute-start | bytes 24584 | tf_op jit(solution)/shard_map/ppermute | solution.py:24
  7.6 11.5 %collective-permute-start.4 = (f32[4,2,2,128]{3,0,2,1:T(4,128)S(1)}, f32[4,2,2,128]{3,0,2,1:T(4,128)S(1)}, u32[]{:S(2)}, u32[]{:S(2)}) collective-permute-start(f32[4,2,2,128]{3,0,2,1:T(4,128)S(1)} %pad_maximum_fusion.7), channel_id=1, source_target_pairs={{0,2},{2,4},{4,6},{6,8},{8,10},{10,12},{12,14},{14,16},{16,18},{18... | collective-permute-start | bytes 24584 | tf_op jit(solution)/shard_map/ppermute | solution.py:21
  7.7 5.8 %collective-permute-start = (s32[1,2,257]{2,1,0:T(2,128)S(1)}, s32[1,2,257]{2,1,0:T(2,128)S(1)}, u32[]{:S(2)}, u32[]{:S(2)}) collective-permute-start(s32[1,2,257]{2,1,0:T(2,128)S(1)} %get-tuple-element.249), channel_id=1, source_target_pairs={{0,2},{2,4},{4,6},{6,8},{8,10},{10,12},{12,14},{14,16},{16,18},{18... | collective-permute-start | bytes 6176 | tf_op jit(solution)/shard_map/ppermute | solution.py:21
  7.8 5.8 %collective-permute-start.1 = (s32[1,2,257]{2,1,0:T(2,128)S(1)}, s32[1,2,257]{2,1,0:T(2,128)S(1)}, u32[]{:S(2)}, u32[]{:S(2)}) collective-permute-start(s32[1,2,257]{2,1,0:T(2,128)S(1)} %get-tuple-element.250), channel_id=1, source_target_pairs={{2,0},{4,2},{6,4},{8,6},{10,8},{12,10},{14,12},{16,14},{18,16},{20... | collective-permute-start | bytes 6176 | tf_op jit(solution)/shard_map/ppermute | solution.py:24
  13.6 3.7 %collective-permute-start.2 = (s32[4,1,257]{2,1,0:T(1,128)S(1)}, s32[4,1,257]{2,1,0:T(1,128)S(1)}, u32[]{:S(2)}, u32[]{:S(2)}) collective-permute-start(s32[4,1,257]{2,1,0:T(1,128)S(1)} %get-tuple-element.232), channel_id=1, source_target_pairs={{0,1},{1,0},{2,3},{3,2},{4,5},{5,4},{6,7},{7,6},{8,9},{9,8},{10,11... | collective-permute-start | bytes 12344 | tf_op jit(solution)/shard_map/ppermute | solution.py:21
  15.2 3.6 %collective-permute-start.3 = (s32[4,1,257]{2,1,0:T(1,128)S(1)}, s32[4,1,257]{2,1,0:T(1,128)S(1)}, u32[]{:S(2)}, u32[]{:S(2)}) collective-permute-start(s32[4,1,257]{2,1,0:T(1,128)S(1)} %get-tuple-element.233), channel_id=1, source_target_pairs={{1,0},{0,1},{3,2},{2,3},{5,4},{4,5},{7,6},{6,7},{9,8},{8,9},{11,10... | collective-permute-start | bytes 12344 | tf_op jit(solution)/shard_map/ppermute | solution.py:24
  19.1 3.9 %collective-permute-start.7 = (f32[4,6,2,128]{3,0,2,1:T(4,128)S(1)}, f32[4,6,2,128]{3,0,2,1:T(4,128)S(1)}, u32[]{:S(2)}, u32[]{:S(2)}) collective-permute-start(f32[4,6,2,128]{3,0,2,1:T(4,128)S(1)} %pad_maximum_fusion.6), channel_id=1, source_target_pairs={{1,0},{0,1},{3,2},{2,3},{5,4},{4,5},{7,6},{6,7},{9,8},{8,9},{11,10... | collective-permute-start | bytes 73736 | tf_op jit(solution)/shard_map/ppermute | solution.py:24
  19.7 3.8 %collective-permute-start.6 = (f32[4,6,2,128]{3,0,2,1:T(4,128)S(1)}, f32[4,6,2,128]{3,0,2,1:T(4,128)S(1)}, u32[]{:S(2)}, u32[]{:S(2)}) collective-permute-start(f32[4,6,2,128]{3,0,2,1:T(4,128)S(1)} %pad_maximum_fusion.6), channel_id=1, source_target_pairs={{0,1},{1,0},{2,3},{3,2},{4,5},{5,4},{6,7},{7,6},{8,9},{9,8},{10,11... | collective-permute-start | bytes 73736 | tf_op jit(solution)/shard_map/ppermute | solution.py:21
  40.0 0.7 copy-start.6
  42.0 0.7 copy-start.2
  50.7 1.1 %copy-start.7 = (f32[128]{0:T(128)S(1)}, f32[128]{0:T(128)}, u32[]{:S(2)}) copy-start(f32[128]{0:T(128)} %param.53) | copy-start | bytes 1540
  52.9 0.7 copy-start.1
  58.8 1.0 %slice-start = ((f32[160,2,2,128]{3,0,2,1:T(8,128)}), f32[128,2,2,128]{3,0,2,1:T(8,128)S(1)}, s32[]{:S(2)}) async-start(f32[160,2,2,128]{3,0,2,1:T(8,128)} %copy-done.1), calls=%async_computation | async-start | bytes 524288 | tf_op jit(solution)/shard_map/transpose(jvp())/split | solution.py:102
  69.9 6.0 %collective-permute-start.8 = (f32[3,2,6,128]{3,0,2,1:T(4,128)S(1)}, f32[3,2,6,128]{3,0,2,1:T(4,128)S(1)}, u32[]{:S(2)}, u32[]{:S(2)}) collective-permute-start(f32[3,2,6,128]{3,0,2,1:T(4,128)S(1)} %get-tuple-element.211), channel_id=1, source_target_pairs={{0,2},{2,4},{4,6},{6,8},{8,10},{10,12},{12,14},{14,16},{16,18},{18... | collective-permute-start | bytes 55304 | tf_op jit(solution)/shard_map/ppermute | solution.py:21
  69.9 6.0 %collective-permute-start.9 = (f32[3,2,6,128]{3,0,2,1:T(4,128)S(1)}, f32[3,2,6,128]{3,0,2,1:T(4,128)S(1)}, u32[]{:S(2)}, u32[]{:S(2)}) collective-permute-start(f32[3,2,6,128]{3,0,2,1:T(4,128)S(1)} %get-tuple-element.212), channel_id=1, source_target_pairs={{2,0},{4,2},{6,4},{8,6},{10,8},{12,10},{14,12},{16,14},{18,16},{20... | collective-permute-start | bytes 55304 | tf_op jit(solution)/shard_map/ppermute | solution.py:24
  75.9 4.1 %collective-permute-start.10 = (f32[3,10,2,128]{3,0,2,1:T(4,128)S(1)}, f32[3,10,2,128]{3,0,2,1:T(4,128)S(1)}, u32[]{:S(2)}, u32[]{:S(2)}) collective-permute-start(f32[3,10,2,128]{3,0,2,1:T(4,128)S(1)} %get-tuple-element.209), channel_id=1, source_target_pairs={{0,1},{1,0},{2,3},{3,2},{4,5},{5,4},{6,7},{7,6},{8,9},{9,8},{10,11... | collective-permute-start | bytes 92168 | tf_op jit(solution)/shard_map/ppermute | solution.py:21
  77.5 4.0 %collective-permute-start.11 = (f32[3,10,2,128]{3,0,2,1:T(4,128)S(1)}, f32[3,10,2,128]{3,0,2,1:T(4,128)S(1)}, u32[]{:S(2)}, u32[]{:S(2)}) collective-permute-start(f32[3,10,2,128]{3,0,2,1:T(4,128)S(1)} %get-tuple-element.210), channel_id=1, source_target_pairs={{1,0},{0,1},{3,2},{2,3},{5,4},{4,5},{7,6},{6,7},{9,8},{8,9},{11,10... | collective-permute-start | bytes 92168 | tf_op jit(solution)/shard_map/ppermute | solution.py:24
where the time goes:
time: 82.5 us; the launch traced here: 82.1 us
  matrix products  42.6 us (52%)
  starting transfers between devices  20.8 us (25%)
  waiting for transfers between devices  10.7 us (13%)
  other arithmetic  3.56 us (4%)
  local copies, waits for them, and re-layouts  3.19 us (4%)
  between operations  1.25 us (2%)
    dot_general x45, matrix products, pick_other(): jnp.einsum('fabn,aben->fabe', block, other_hot, precision=HIGH) * chosen  29 us
    ppermute x6, starting transfers between devices, extended_2(): lax.ppermute(lax.slice_in_dim(block, 0, width, axis=dim), axis, backward)  16 us
    ppermute x6, waiting for transfers between devices, extended_2(): lax.ppermute(lax.slice_in_dim(block, block.shape[dim] - width, None, axis...  5.85 us
    ppermute x6, waiting for transfers between devices, extended_2(): lax.ppermute(lax.slice_in_dim(block, 0, width, axis=dim), axis, backward)  4.89 us
    ppermute x6, starting transfers between devices, extended_2(): lax.ppermute(lax.slice_in_dim(block, block.shape[dim] - width, None, axis...  4.81 us
    dot_general x2, matrix products, features(): jnp.einsum('fabe,aben->fabn', messages, one_hot, precision=HIGH)  3.27 us
    dot_general x5, matrix products, pick_center(): return jnp.einsum('fabn,aben->fabe', lattice, center_hot, precision=HIGH)  3.19 us
    unnamed x19, local copies, waits for them, and re-layouts  2.76 us
  transfers between devices with their start and end apart: 12, of which 9 were waited for; matrix products, arithmetic and copies ran while one was open for 2% of the time, Pallas kernels for 0%

commit v1 on v0

v1 whole, which is shorter than its diff:
```python
import functools
import math

import jax
import jax.numpy as jnp
from jax import lax
from jax.experimental import pallas as pl
from jax.experimental.pallas import tpu as pltpu
from jax.sharding import PartitionSpec as P

SOFTEN = 0.01
CUTOFF = 3.5
F32 = jnp.float32
BF16 = jnp.bfloat16
MESH = pl.DeviceIdType.MESH


def rounded(x):
    return x.astype(BF16).astype(F32)


def split(x):
    high = x.astype(BF16)
    return high, (x - high.astype(F32)).astype(BF16)


def dot(a, b):
    return jnp.dot(a, b, preferred_element_type=F32)


def dot_t(a, b):
    return lax.dot_general(a, b, (((1,), (1,)), ((), ())), preferred_element_type=F32)


def join(parts, axis):
    return parts[0] if len(parts) == 1 else jnp.concatenate(parts, axis=axis)


def neighbours(nz, nx):
    slots = {(0, 0): 0}
    for dz in (-1, 0, 1):
        for dx in (-1, 0, 1):
            slots.setdefault((dz % nz, dx % nx), len(slots))
    return slots


def kernel(
    nz, nx, bz, bx, nb, spec, ch, lat,
    coords_ref, species_ref, centers_ref, others_ref, live_ref, in_ref, env_ref, up_ref, out_ref,
    energy_ref, forces_ref,
    own, halo, tab, ct, ot, rows_live, rows_p, geo, xs, sins, coss, rad, harm,
    l2, dsilu, wts, feat, dfeat, dlat_own, env_grad, dharm, drad, gr, grad, back,
    send1, recv1, send2, recv2,
):
    n = coords_ref.shape[-1]
    slots = neighbours(nz, nx)
    me_z, me_x = lax.axis_index("gz"), lax.axis_index("xy")
    others_list = [(key, s) for key, s in slots.items() if s > 0]

    def device(key):
        return (lax.rem(me_z + key[0], nz), lax.rem(me_x + key[1], nx))

    def mirror(key):
        return slots[((-key[0]) % nz, (-key[1]) % nx)]

    barrier = pltpu.get_barrier_semaphore()
    for key, _ in others_list:
        pl.semaphore_signal(barrier, inc=1, device_id=device(key), device_id_type=MESH)

    lane = lax.broadcasted_iota(jnp.int32, (1, n), 1)
    for a in range(bz):
        for b in range(bx):
            alive = (lane < live_ref[a, b]).astype(F32)
            own[a, b] = jnp.concatenate(
                [
                    coords_ref[:, a, b, :],
                    species_ref[a, b : b + 1, :].astype(F32),
                    centers_ref[a, b : b + 1, :].astype(F32),
                    others_ref[a, b : b + 1, :].astype(F32),
                    alive,
                    jnp.zeros((1, n), F32),
                ],
                axis=0,
            )
    pl.semaphore_wait(barrier, len(others_list))
    first = []
    for key, s in others_list:
        t = mirror(key)
        copy = pltpu.make_async_remote_copy(
            src_ref=own, dst_ref=halo.at[t - 1], send_sem=send1.at[s - 1],
            recv_sem=recv1.at[t - 1], device_id=device(key), device_id_type=MESH,
        )
        copy.start()
        first.append(copy)

    w_in = in_ref[...]
    w_hi = rounded(w_in)
    w_lo = w_in - w_hi
    w_rows = jnp.concatenate(
        [w_hi[:nb], w_lo[:nb], w_hi[:nb], w_hi[nb:], w_lo[nb:],
         jnp.zeros((lat - 3 * nb - 4 * spec, lat), F32)], axis=0)
    kin = (3 * nb + 4 * spec + 15) // 16 * 16
    in_t = w_rows.T.astype(BF16)[:, :kin]
    pad8 = jnp.zeros((nb, lat), F32)
    wr_hi = jnp.concatenate([w_hi[:nb], pad8], axis=0).astype(BF16)
    wr_lo = jnp.concatenate([w_lo[:nb], pad8], axis=0).astype(BF16)
    wr3 = jnp.concatenate([wr_hi, wr_hi, wr_lo], axis=1)
    env_t = env_ref[...].T
    et_hi = rounded(env_t)
    et_lo = env_t - et_hi
    env_t3 = jnp.concatenate([et_hi, et_hi, et_lo], axis=1).astype(BF16)
    kpad = -(3 * ch) % lat
    env3 = jnp.concatenate(
        [et_hi, et_hi, et_lo] + ([jnp.zeros((kpad, lat), F32)] if kpad else []), axis=0
    ).T.astype(BF16)
    up = up_ref[...]
    up_hi = rounded(up)
    up_lo = up - up_hi
    up3 = jnp.concatenate([up_hi, up_hi, up_lo], axis=1).astype(BF16)
    up_t = jnp.concatenate(
        [x.T.astype(BF16) for x in (up_hi[:lat], up_hi[:lat], up_lo[:lat])]
        + [jnp.concatenate(
            [up_hi[lat:], up_hi[lat:], up_lo[lat:]]
            + ([jnp.zeros((kpad, lat), F32)] if kpad else []), axis=0).T.astype(BF16)],
        axis=1)
    out_col = jnp.broadcast_to(out_ref[...], (n, lat)).T

    for copy in first:
        copy.wait()

    def place(a, b):
        return slots[((a // bz - 1) % nz, (b // bx - 1) % nx)], a % bz, b % bx

    def block(a, b):
        s, i, j = place(a, b)
        return own[i, j] if s == 0 else halo[s - 1, i, j]

    window_z = range(bz - 2, 2 * bz + 2)
    window_x = range(bx - 2, 2 * bx + 2)
    for a in window_z:
        for b in window_x:
            part = block(a, b)
            hi = rounded(part)
            tab[a, b] = jnp.concatenate([hi, part - hi], axis=0).astype(BF16)

    cells = [(a, b) for a in range(bz - 1, 2 * bz + 1) for b in range(bx - 1, 2 * bx + 1)]
    cx = bx + 2
    total = len(cells)
    row_n = lax.broadcasted_iota(jnp.int32, (n, n), 0)
    row_s = lax.broadcasted_iota(jnp.int32, (spec, n), 0).astype(F32)
    for i, (a, b) in enumerate(cells):
        part = block(a, b)
        c = part[4:5].astype(jnp.int32)
        o = part[5:6].astype(jnp.int32)
        p = o >> 7
        hot_c = (row_n == c).astype(F32).astype(BF16)
        hot_o = (row_n == (o & 127)).astype(F32).astype(BF16)
        ct[i] = hot_c
        ot[i] = hot_o
        at_c = dot(tab[a, b], hot_c)
        at_c = at_c[:8] + at_c[8:]
        around = jnp.concatenate(
            [tab[a + dz, b + dx] for dz in (-1, 0, 1) for dx in (-1, 0, 1)], axis=0)
        got = dot(around, hot_o)
        at_o = jnp.zeros((8, n), F32)
        for off in range(9):
            at_o = jnp.where(p == off, got[16 * off : 16 * off + 8] + got[16 * off + 8 : 16 * off + 16], at_o)
        diff = at_o - at_c
        up3_ = (p >= 3).astype(jnp.int32) + (p >= 6).astype(jnp.int32)
        geo[0, i : i + 1] = diff[0:1] + (up3_ - 1).astype(F32)
        geo[1, i : i + 1] = diff[1:2] + (p - 3 * up3_ - 1).astype(F32)
        geo[2, i : i + 1] = diff[2:3]
        xs[:spec, i * n : (i + 1) * n] = (row_s == at_c[3:4]).astype(F32)
        xs[spec:, i * n : (i + 1) * n] = (row_s == at_o[3:4]).astype(F32)
        rows_live[i : i + 1] = part[6:7]
        rows_p[i : i + 1] = p

    r = [geo[m] for m in range(3)]
    dist = jnp.sqrt(r[0] * r[0] + r[1] * r[1] + r[2] * r[2] + SOFTEN)
    inv = 1.0 / dist
    q = dist / CUTOFF
    rest = 1.0 - q * q
    envelope = rest * rest
    scale = inv * envelope
    s1 = jnp.sin(math.pi * q)
    c1 = jnp.cos(math.pi * q)
    s0, c0, sk, ck = jnp.zeros_like(s1), jnp.ones_like(c1), s1, c1
    for k in range(nb):
        sins[k] = sk
        coss[k] = ck
        rad[k] = sk * scale
        s0, sk = sk, 2.0 * c1 * sk - s0
        c0, ck = ck, 2.0 * c1 * ck - c0
    for m in range(3):
        harm[m] = r[m] * inv
    env_grad[...] = jnp.zeros_like(env_grad)
    geo[3] = envelope

    interior = {}
    for i, (a, b) in enumerate(cells):
        if bz <= a < 2 * bz and bx <= b < 2 * bx:
            interior[i] = (a - bz) * bx + (b - bx)

    group = 2 if total % 2 == 0 else 1
    for g in range(0, total, group):
        ids = list(range(g, g + group))
        span = slice(g * n, (g + group) * n)
        radial = join([rad[:, i, :] for i in ids], 1)
        rh = rounded(radial)
        x_s = xs[:, span]
        parts = [rh, rh, radial - rh, x_s, x_s]
        fill = kin - 3 * nb - 4 * spec
        if fill:
            parts.append(jnp.zeros((fill, group * n), F32))
        pre = dot(in_t, jnp.concatenate(parts, axis=0).astype(BF16))
        sig = 1.0 / (1.0 + jnp.exp(-pre))
        latent = pre * sig
        dsilu[:, span] = sig + latent * (1.0 - sig)
        lh, ll = split(latent)
        for t, i in enumerate(ids):
            if i in interior:
                l2[interior[i], 0] = lh[:, t * n : (t + 1) * n]
                l2[interior[i], 1] = ll[:, t * n : (t + 1) * n]
        alive = join([rows_live[i : i + 1] for i in ids], 1)
        w = dot(env_t3, jnp.concatenate([lh, ll, lh], axis=0)) * alive
        wts[:, span] = w
        msgs = jnp.concatenate(
            [w] + [w * join([harm[m, i : i + 1] for i in ids], 1) for m in range(3)], axis=0)
        mh, ml = split(msgs)
        for t, i in enumerate(ids):
            cut = slice(t * n, (t + 1) * n)
            hot_c = ct[i]
            feat[:, i * n : (i + 1) * n] = dot_t(
                jnp.concatenate([mh[:, cut], ml[:, cut]], axis=1),
                jnp.concatenate([hot_c, hot_c], axis=1)).astype(BF16)

    dfeat[...] = jnp.zeros_like(dfeat)
    row_8 = lax.broadcasted_iota(jnp.int32, (16, n), 0)
    for i, k in interior.items():
        hot_c, hot_o = ct[i], ot[i]
        p = rows_p[i : i + 1]
        env_row = geo[3, i : i + 1]
        alive = rows_live[i : i + 1]
        f_c = dot(feat[:, i * n : (i + 1) * n], hot_c)
        f_o = None
        hots = []
        for dz in range(3):
            start = i + (dz - 1) * cx - 1
            hot3 = jnp.concatenate(
                [hot_o * (p == 3 * dz + dx).astype(F32).astype(BF16) for dx in range(3)], axis=0)
            hots.append((start, hot3))
            term = dot(feat[:, start * n : (start + 3) * n], hot3)
            f_o = term if f_o is None else f_o + term
        prod4 = f_c * f_o
        prod = prod4[:ch] + prod4[ch : 2 * ch] + prod4[2 * ch : 3 * ch] + prod4[3 * ch :]
        ph, pl_ = split(prod)
        parts = [l2[k, 0], l2[k, 1], l2[k, 0], ph, pl_, ph]
        if kpad:
            parts.append(jnp.zeros((kpad, n), BF16))
        u = dot(up_t, jnp.concatenate(parts, axis=0))
        sig = 1.0 / (1.0 + jnp.exp(-u))
        hid = u * sig
        raw = jnp.sum(out_col * hid, axis=0, keepdims=True) * alive
        env_grad[i : i + 1] = raw
        e_row = raw * env_row
        e_hi = rounded(e_row)
        e_rows = jnp.where(row_8 == 0, e_hi, jnp.where(row_8 == 1, e_row - e_hi, 0.0)).astype(BF16)
        e_atom = dot_t(e_rows, hot_c)
        energy_ref[k // bx, k % bx : k % bx + 1, :] = e_atom[0:1] + e_atom[1:2]
        d_u = out_col * (alive * env_row) * (sig + hid * (1.0 - sig))
        dh, dl = split(d_u)
        d_join = dot(up3, jnp.concatenate([dh, dl, dh], axis=0))
        dlat_own[k] = d_join[:lat]
        d_prod = jnp.concatenate([d_join[lat:]] * 4, axis=0)
        dch, dcl = split(d_prod * f_o)
        doh, dol = split(d_prod * f_c)
        dfeat[:, i * n : (i + 1) * n] += dot_t(
            jnp.concatenate([dch, dcl], axis=1), jnp.concatenate([hot_c, hot_c], axis=1))
        d_o = jnp.concatenate([doh, dol], axis=1)
        for start, hot3 in hots:
            dfeat[:, start * n : (start + 3) * n] += dot_t(
                d_o, jnp.concatenate([hot3, hot3], axis=1))

    for g in range(0, total, group):
        ids = list(range(g, g + group))
        span = slice(g * n, (g + group) * n)
        dm = []
        for i in ids:
            hot_c = ct[i]
            fh, fl = split(dfeat[:, i * n : (i + 1) * n])
            dm.append(dot(jnp.concatenate([fh, fl], axis=1), jnp.concatenate([hot_c, hot_c], axis=0)))
        dm = join(dm, 1)
        w = wts[:, span]
        dw = dm[:ch]
        for m in range(3):
            piece = dm[(m + 1) * ch : (m + 2) * ch]
            dw = dw + piece * join([harm[m, i : i + 1] for i in ids], 1)
            d_h = jnp.sum(piece * w, axis=0, keepdims=True)
            for t, i in enumerate(ids):
                dharm[m, i : i + 1] = d_h[:, t * n : (t + 1) * n]
        dw = dw * join([rows_live[i : i + 1] for i in ids], 1)
        wh, wl = split(dw)
        parts = [wh, wl, wh]
        if kpad:
            parts.append(jnp.zeros((kpad, group * n), BF16))
        d_lat = dot(env3, jnp.concatenate(parts, axis=0))
        if any(i in interior for i in ids):
            d_lat = d_lat + join(
                [dlat_own[interior[i]] if i in interior else jnp.zeros((lat, n), F32) for i in ids], 1)
        dh, dl = split(d_lat * dsilu[:, span])
        d_r = dot(wr3, jnp.concatenate([dh, dl, dh], axis=0))
        for t, i in enumerate(ids):
            drad[:, i, :] = d_r[:nb, t * n : (t + 1) * n]

    sum_s = drad[0] * sins[0]
    sum_c = drad[0] * coss[0]
    for k in range(1, nb):
        sum_s = sum_s + drad[k] * sins[k]
        sum_c = sum_c + (k + 1.0) * (drad[k] * coss[k])
    env_slope = (-4.0 / CUTOFF) * q * rest
    d_dist = (
        (math.pi / CUTOFF) * sum_c * scale
        - sum_s * scale * inv
        + (sum_s * inv + env_grad[...]) * env_slope
    )
    for m in range(3):
        d_dist = d_dist - dharm[m] * r[m] * (inv * inv)
    gr[...] = jnp.zeros_like(gr)
    for m in range(3):
        d_m = d_dist * harm[m] + dharm[m] * inv
        hi = rounded(d_m)
        gr[:, m, :] = hi
        gr[:, m + 4, :] = d_m - hi

    grad[...] = jnp.zeros_like(grad)
    for i, (a, b) in enumerate(cells):
        g8 = gr[i]
        p = rows_p[i : i + 1]
        at_c = dot_t(jnp.concatenate([g8, jnp.zeros_like(g8)], axis=0).astype(BF16), ct[i])
        stack = [jnp.where(p == off, g8, 0.0) for off in range(9)] + [jnp.zeros_like(g8)]
        at_o = dot_t(jnp.concatenate(stack, axis=0).astype(BF16), ot[i])
        s, y, x = place(a, b)
        grad[s, y, x] -= at_c[:8]
        for off in range(9):
            s, y, x = place(a + off // 3 - 1, b + off % 3 - 1)
            grad[s, y, x] += at_o[8 * off : 8 * off + 8]

    second = []
    for key, s in others_list:
        t = mirror(key)
        copy = pltpu.make_async_remote_copy(
            src_ref=grad.at[s], dst_ref=back.at[t - 1], send_sem=send2.at[s - 1],
            recv_sem=recv2.at[t - 1], device_id=device(key), device_id_type=MESH,
        )
        copy.start()
        second.append(copy)
    for copy in second:
        copy.wait()
    for a in range(bz):
        for b in range(bx):
            acc = grad[0, a, b]
            for s in range(len(others_list)):
                acc = acc + back[s, a, b]
            acc = -(acc[:4] + acc[4:])
            forces_ref[:, a, b, :] = acc[:3]


def solution(mesh):
    nz, nx = mesh.shape["gz"], mesh.shape["xy"]

    def body(coords, species, centers, others, live_count, in_weight, env_weight, up_weight, out_weight):
        _, bz, bx, n = coords.shape
        lat, ch = env_weight.shape
        nb = 8
        spec = (in_weight.shape[0] - nb) // 2
        cells = (bz + 2) * (bx + 2)
        ns = len(neighbours(nz, nx)) - 1
        vmem = lambda shape, dtype=F32: pltpu.VMEM(shape, dtype)
        scratch = [
            vmem((bz, bx, 8, n)),
            vmem((ns, bz, bx, 8, n)),
            vmem((3 * bz, 3 * bx, 16, n), BF16),
            vmem((cells, n, n), BF16),
            vmem((cells, n, n), BF16),
            vmem((cells, n)),
            vmem((cells, n), jnp.int32),
            vmem((4, cells, n)),
            vmem((2 * spec, cells * n)),
            vmem((nb, cells, n)),
            vmem((nb, cells, n)),
            vmem((nb, cells, n)),
            vmem((3, cells, n)),
            vmem((bz * bx, 2, lat, n), BF16),
            vmem((lat, cells * n)),
            vmem((ch, cells * n)),
            vmem((4 * ch, cells * n), BF16),
            vmem((4 * ch, cells * n)),
            vmem((bz * bx, lat, n)),
            vmem((cells, n)),
            vmem((3, cells, n)),
            vmem((nb, cells, n)),
            vmem((cells, 8, n)),
            vmem((ns + 1, bz, bx, 8, n)),
            vmem((ns, bz, bx, 8, n)),
        ] + [pltpu.SemaphoreType.DMA((ns,)) for _ in range(4)]
        specs = [pl.BlockSpec(memory_space=pltpu.VMEM) for _ in range(9)]
        specs[4] = pl.BlockSpec(memory_space=pltpu.SMEM)
        return pl.pallas_call(
            functools.partial(kernel, nz, nx, bz, bx, nb, spec, ch, lat),
            out_shape=(
                jax.ShapeDtypeStruct((bz, bx, n), F32),
                jax.ShapeDtypeStruct((3, bz, bx, n), F32),
            ),
            in_specs=specs,
            out_specs=(pl.BlockSpec(memory_space=pltpu.VMEM), pl.BlockSpec(memory_space=pltpu.VMEM)),
            scratch_shapes=scratch,
            compiler_params=pltpu.CompilerParams(collective_id=0, has_side_effects=True),
        )(coords, species, centers, others, live_count, in_weight, env_weight, up_weight, out_weight[None])

    in_specs = (
        P(None, "gz", "xy", None), P("gz", "xy", None), P("gz", "xy", None), P("gz", "xy", None),
        P("gz", "xy"), P(), P(), P(), P(),
    )
    out_specs = (P("gz", "xy", None), P(None, "gz", "xy", None))
    return jax.shard_map(body, mesh=mesh, in_specs=in_specs, out_specs=out_specs, check_vma=False)
```

time: 82.5 us -> 30.4 us (0.37)
  matrix products: 42.6 us -> 0 us
  Pallas kernels: 0 us -> 26.2 us
  starting transfers between devices: 20.8 us -> 0 us
  waiting for transfers between devices: 10.7 us -> 0 us
  other arithmetic: 3.56 us -> 0 us
    dot_general x60 -> x0, matrix products: 42.6 us -> none  [the longest x45 29 us: pick_other(): jnp.einsum('fabn,aben->fabe', block, other_hot, precision=HIGH) * chosen]
    pallas_call x0 -> x1, Pallas kernels: none -> 26.2 us  [body(): pl.pallas_call(functools.partial(kernel, nz, nx, bz, bx, nb, spec, ch, la...]
    ppermute x12 -> x0, starting transfers between devices: 20.8 us -> none  [the longest x6 16 us: extended_2(): lax.ppermute(lax.slice_in_dim(block, 0, width, axis=dim), axis, backward)]
    ppermute x12 -> x0, waiting for transfers between devices: 10.7 us -> none  [the longest x6 5.85 us: extended_2(): lax.ppermute(lax.slice_in_dim(block, block.shape[dim] - width, None, axis...]
    reduce_sum x3 -> x0, other arithmetic: 1.41 us -> none  [the longest x1 0.86 us: features(): weights[:, None] * harmonics[None]]
    convert_element_type x7 -> x0, other arithmetic: 0.87 us -> none  [the longest x1 0.72 us: body(): species.astype(jnp.float32)[None]]
    unnamed x19 -> x5, local copies, waits for them, and re-layouts: 2.76 us -> 3.29 us
  transfers between devices with their start and end apart: 12 -> 0, of which waited for: 9 -> 0; matrix products, arithmetic and copies ran while one was open for 2% -> 0% of each run, Pallas kernels for 0% -> 0%
where the time goes in v1:
time: 30.4 us; the launch traced here: 30.2 us
  Pallas kernels  26.2 us (86%)
  local copies, waits for them, and re-layouts  3.29 us (11%)
  between operations  0.65 us (2%)
    pallas_call x1, Pallas kernels, body(): pl.pallas_call(functools.partial(kernel, nz, nx, bz, bx, nb, spec, ch, la...  26.2 us
    unnamed x5, local copies, waits for them, and re-layouts  3.29 us

profile of v1, /device:TPU:0, one launch (start us, length us, event | category | flops | bytes accessed | tf_op | source)
XLA Modules:
  0.0 30.2 jit_solution(4692050130171522768)
XLA Ops:
  0.6 1.4 %copy.11.env_ref = f32[128,32]{1,0:T(8,128)} copy(f32[128,32]{0,1:T(8,128)} %param.15) | data formatting | bytes 32768 | tf_op args[6]
  2.1 26.2 %shard_map.104 = (f32[2,2,128]{2,1,0:T(2,128)}, f32[3,2,2,128]{3,2,1,0:T(2,128)}) custom-call(f32[3,2,2,128]{3,2,1,0:T(2,128)} %coords_ref.1, s32[2,2,128]{2,1,0:T(2,128)} %species_ref.1, s32[2,2,128]{2,1,0:T(2,128)} %centers_ref.1, s32[2,2,128]{2,1,0:T(2,128)} %others_ref.1, s32[2,2]{1,0:T(2,128)} %live_ref.1, f32[24,128]{1,0:T(8,128)} %in_ref.1, ...), custom_call_target="tpu_custom_call" | custom-call | tf_op jit(solution)/shard_map/pallas_call | solution.py:408
  28.3 0.0 copy-start
  28.3 1.3 %copy.14 = f32[2,2,128]{2,1,0:T(2,128)} copy(f32[2,2,128]{2,1,0:T(2,128)} %get-tuple-element.4) | data formatting | bytes 4096
  29.6 0.0 copy-done
  29.6 0.6 %copy.15 = f32[3,2,2,128]{3,2,1,0:T(2,128)} copy(f32[3,2,2,128]{3,2,1,0:T(2,128)S(1)} %copy-done) | data formatting | bytes 12288
Async XLA Ops:
  28.3 1.3 %copy-start = (f32[3,2,2,128]{3,2,1,0:T(2,128)S(1)}, f32[3,2,2,128]{3,2,1,0:T(2,128)}, u32[]{:S(2)}) copy-start(f32[3,2,2,128]{3,2,1,0:T(2,128)} %get-tuple-element.5) | copy-start | bytes 18436

commit v2 on v1

--- a/solution.py
+++ b/solution.py
@@ -47,7 +47,7 @@
 def kernel(
     nz, nx, bz, bx, nb, spec, ch, lat,
     coords_ref, species_ref, centers_ref, others_ref, live_ref, in_ref, env_ref, up_ref, out_ref,
-    energy_ref, forces_ref,
+    result_ref,
     own, halo, tab, ct, ot, rows_live, rows_p, geo, xs, sins, coss, rad, harm,
     l2, dsilu, wts, feat, dfeat, dlat_own, env_grad, dharm, drad, gr, grad, back,
     send1, recv1, send2, recv2,
@@ -105,7 +105,7 @@
     wr_hi = jnp.concatenate([w_hi[:nb], pad8], axis=0).astype(BF16)
     wr_lo = jnp.concatenate([w_lo[:nb], pad8], axis=0).astype(BF16)
     wr3 = jnp.concatenate([wr_hi, wr_hi, wr_lo], axis=1)
-    env_t = env_ref[...].T
+    env_t = env_ref[...]
     et_hi = rounded(env_t)
     et_lo = env_t - et_hi
     env_t3 = jnp.concatenate([et_hi, et_hi, et_lo], axis=1).astype(BF16)
@@ -266,7 +266,7 @@
         e_hi = rounded(e_row)
         e_rows = jnp.where(row_8 == 0, e_hi, jnp.where(row_8 == 1, e_row - e_hi, 0.0)).astype(BF16)
         e_atom = dot_t(e_rows, hot_c)
-        energy_ref[k // bx, k % bx : k % bx + 1, :] = e_atom[0:1] + e_atom[1:2]
+        result_ref[3, k // bx, k % bx : k % bx + 1, :] = e_atom[0:1] + e_atom[1:2]
         d_u = out_col * (alive * env_row) * (sig + hid * (1.0 - sig))
         dh, dl = split(d_u)
         d_join = dot(up3, jnp.concatenate([dh, dl, dh], axis=0))
@@ -362,7 +362,7 @@
             for s in range(len(others_list)):
                 acc = acc + back[s, a, b]
             acc = -(acc[:4] + acc[4:])
-            forces_ref[:, a, b, :] = acc[:3]
+            result_ref[:3, a, b, :] = acc[:3]
 
 
 def solution(mesh):
@@ -405,17 +405,15 @@
         ] + [pltpu.SemaphoreType.DMA((ns,)) for _ in range(4)]
         specs = [pl.BlockSpec(memory_space=pltpu.VMEM) for _ in range(9)]
         specs[4] = pl.BlockSpec(memory_space=pltpu.SMEM)
-        return pl.pallas_call(
+        result = pl.pallas_call(
             functools.partial(kernel, nz, nx, bz, bx, nb, spec, ch, lat),
-            out_shape=(
-                jax.ShapeDtypeStruct((bz, bx, n), F32),
-                jax.ShapeDtypeStruct((3, bz, bx, n), F32),
-            ),
+            out_shape=jax.ShapeDtypeStruct((4, bz, bx, n), F32),
             in_specs=specs,
-            out_specs=(pl.BlockSpec(memory_space=pltpu.VMEM), pl.BlockSpec(memory_space=pltpu.VMEM)),
+            out_specs=pl.BlockSpec(memory_space=pltpu.VMEM),
             scratch_shapes=scratch,
             compiler_params=pltpu.CompilerParams(collective_id=0, has_side_effects=True),
-        )(coords, species, centers, others, live_count, in_weight, env_weight, up_weight, out_weight[None])
+        )(coords, species, centers, others, live_count, in_weight, env_weight.T, up_weight, out_weight[None])
+        return result[3], result[:3]
 
     in_specs = (
         P(None, "gz", "xy", None), P("gz", "xy", None), P("gz", "xy", None), P("gz", "xy", None),

time: 30.4 us -> 29.6 us (0.974)
  local copies, waits for them, and re-layouts: 3.29 us -> 2.53 us
    unnamed x5 -> x0, local copies, waits for them, and re-layouts: 3.29 us -> none
    slice x0 -> x1, local copies, waits for them, and re-layouts: none -> 1.28 us  [body(): return (result[3], result[:3])]
    squeeze x0 -> x1, local copies, waits for them, and re-layouts: none -> 1.25 us  [body(): return (result[3], result[:3])]
where the time goes in v2:
time: 29.6 us; the launch traced here: 29.4 us
  Pallas kernels  26.2 us (89%)
  local copies, waits for them, and re-layouts  2.53 us (9%)
  between operations  0.64 us (2%)
    pallas_call x1, Pallas kernels, body(): pl.pallas_call(functools.partial(kernel, nz, nx, bz, bx, nb, spec, ch, la...  26.2 us
    slice x1, local copies, waits for them, and re-layouts, body(): return (result[3], result[:3])  1.28 us
    squeeze x1, local copies, waits for them, and re-layouts, body(): return (result[3], result[:3])  1.25 us

profile of v2, /device:TPU:0, one launch (start us, length us, event | category | flops | bytes accessed | tf_op | source)
XLA Modules:
  0.0 29.4 jit_solution(11325563173909950911)
XLA Ops:
  0.6 26.2 %shard_map.104 = f32[4,2,2,128]{3,2,1,0:T(2,128)} custom-call(f32[3,2,2,128]{3,2,1,0:T(2,128)} %coords_ref.1, s32[2,2,128]{2,1,0:T(2,128)} %species_ref.1, s32[2,2,128]{2,1,0:T(2,128)} %centers_ref.1, s32[2,2,128]{2,1,0:T(2,128)} %others_ref.1, s32[2,2]{1,0:T(2,128)} %live_ref.1, f32[24,128]{1,0:T(8,128)} %in_ref.1, f32[32,128]{1,0:T(8,128)} %bitcast.4, ...), custom_call_target="tpu_custom_call" | custom-call | tf_op jit(solution)/shard_map/pallas_call | solution.py:408
  26.9 1.2 %slice_bitcast_fusion = f32[2,2,128]{2,1,0:T(2,128)} fusion(f32[4,2,2,128]{3,2,1,0:T(2,128)} %shard_map.104), kind=kLoop, calls=%fused_computation | loop fusion | bytes 4096 | tf_op jit(solution)/shard_map/squeeze | solution.py:416
  28.1 1.3 %slice.7 = f32[3,2,2,128]{3,2,1,0:T(2,128)} slice(f32[4,2,2,128]{3,2,1,0:T(2,128)} %shard_map.104), slice={[0:3], [0:2], [0:2], [0:128]} | slice | bytes 12288 | tf_op jit(solution)/shard_map/slice | solution.py:416

commit v3 on v2

--- a/solution.py
+++ b/solution.py
@@ -46,11 +46,12 @@
 
 def kernel(
     nz, nx, bz, bx, nb, spec, ch, lat,
+    coords_hbm, species_hbm, centers_hbm, others_hbm, live_hbm, in_hbm, env_hbm, up_hbm, out_hbm,
+    result_ref,
     coords_ref, species_ref, centers_ref, others_ref, live_ref, in_ref, env_ref, up_ref, out_ref,
-    result_ref,
     own, halo, tab, ct, ot, rows_live, rows_p, geo, xs, sins, coss, rad, harm,
     l2, dsilu, wts, feat, dfeat, dlat_own, env_grad, dharm, drad, gr, grad, back,
-    send1, recv1, send2, recv2,
+    send1, recv1, send2, recv2, load_sem,
 ):
     n = coords_ref.shape[-1]
     slots = neighbours(nz, nx)
@@ -67,10 +68,21 @@
     for key, _ in others_list:
         pl.semaphore_signal(barrier, inc=1, device_id=device(key), device_id_type=MESH)
 
+    loads = [
+        pltpu.make_async_copy(source, target, load_sem.at[k])
+        for k, (source, target) in enumerate([
+            (coords_hbm, coords_ref), (species_hbm, species_ref), (centers_hbm, centers_ref),
+            (others_hbm, others_ref), (live_hbm, live_ref), (in_hbm, in_ref), (env_hbm, env_ref),
+            (up_hbm, up_ref), (out_hbm, out_ref)])
+    ]
+    for load in loads:
+        load.start()
+    for load in loads[:5]:
+        load.wait()
     lane = lax.broadcasted_iota(jnp.int32, (1, n), 1)
     for a in range(bz):
         for b in range(bx):
-            alive = (lane < live_ref[a, b]).astype(F32)
+            alive = (lane < live_ref[a : a + 1, b : b + 1]).astype(F32)
             own[a, b] = jnp.concatenate(
                 [
                     coords_ref[:, a, b, :],
@@ -93,6 +105,8 @@
         copy.start()
         first.append(copy)
 
+    for load in loads[5:]:
+        load.wait()
     w_in = in_ref[...]
     w_hi = rounded(w_in)
     w_lo = w_in - w_hi
@@ -376,7 +390,9 @@
         cells = (bz + 2) * (bx + 2)
         ns = len(neighbours(nz, nx)) - 1
         vmem = lambda shape, dtype=F32: pltpu.VMEM(shape, dtype)
-        scratch = [
+        args = (coords, species, centers, others, live_count, in_weight, env_weight.T, up_weight,
+                out_weight[None])
+        scratch = [vmem(x.shape, x.dtype) for x in args] + [
             vmem((bz, bx, 8, n)),
             vmem((ns, bz, bx, 8, n)),
             vmem((3 * bz, 3 * bx, 16, n), BF16),
@@ -403,16 +419,16 @@
             vmem((ns + 1, bz, bx, 8, n)),
             vmem((ns, bz, bx, 8, n)),
         ] + [pltpu.SemaphoreType.DMA((ns,)) for _ in range(4)]
-        specs = [pl.BlockSpec(memory_space=pltpu.VMEM) for _ in range(9)]
-        specs[4] = pl.BlockSpec(memory_space=pltpu.SMEM)
+        scratch.append(pltpu.SemaphoreType.DMA((len(args),)))
+        specs = [pl.BlockSpec(memory_space=pl.ANY) for _ in args]
         result = pl.pallas_call(
             functools.partial(kernel, nz, nx, bz, bx, nb, spec, ch, lat),
-            out_shape=jax.ShapeDtypeStruct((4, bz, bx, n), F32),
+            out_shape=pltpu.VMEM((4, bz, bx, n), F32),
             in_specs=specs,
             out_specs=pl.BlockSpec(memory_space=pltpu.VMEM),
             scratch_shapes=scratch,
             compiler_params=pltpu.CompilerParams(collective_id=0, has_side_effects=True),
-        )(coords, species, centers, others, live_count, in_weight, env_weight.T, up_weight, out_weight[None])
+        )(*args)
         return result[3], result[:3]
 
     in_specs = (

time: 29.6 us -> 26.7 us (0.902)
  Pallas kernels: 26.2 us -> 24.7 us
  local copies, waits for them, and re-layouts: 2.53 us -> 1.17 us
    pallas_call x1, Pallas kernels: 26.2 us -> 24.7 us  [body(): pl.pallas_call(functools.partial(kernel, nz, nx, bz, bx, nb, spec, ch, la...]
    slice x1, local copies, waits for them, and re-layouts: 1.28 us -> 0.59 us  [body(): return (result[3], result[:3])]
    squeeze x1, local copies, waits for them, and re-layouts: 1.25 us -> 0.58 us  [body(): return (result[3], result[:3])]
where the time goes in v3:
time: 26.7 us; the launch traced here: 26.6 us
  Pallas kernels  24.7 us (93%)
  local copies, waits for them, and re-layouts  1.17 us (4%)
  between operations  0.64 us (2%)
    pallas_call x1, Pallas kernels, body(): pl.pallas_call(functools.partial(kernel, nz, nx, bz, bx, nb, spec, ch, la...  24.7 us
    slice x1, local copies, waits for them, and re-layouts, body(): return (result[3], result[:3])  0.59 us
    squeeze x1, local copies, waits for them, and re-layouts, body(): return (result[3], result[:3])  0.58 us

profile of v3, /device:TPU:0, one launch (start us, length us, event | category | flops | bytes accessed | tf_op | source)
XLA Modules:
  0.0 26.6 jit_solution(17713801222673218087)
XLA Ops:
  0.6 24.7 %shard_map.104 = f32[4,2,2,128]{3,2,1,0:T(2,128)S(1)} custom-call(f32[3,2,2,128]{3,2,1,0:T(2,128)} %coords_hbm.1, s32[2,2,128]{2,1,0:T(2,128)} %species_hbm.1, s32[2,2,128]{2,1,0:T(2,128)} %centers_hbm.1, s32[2,2,128]{2,1,0:T(2,128)} %others_hbm.1, s32[2,2]{1,0:T(2,128)} %live_hbm.1, f32[24,128]{1,0:T(8,128)} %in_hbm.1, f32[32,128]{1,0:T(8,128)} %bitcast.4, ...), custom_call_target="tpu_custom_call" | custom-call | tf_op jit(solution)/shard_map/pallas_call | solution.py:424
  25.4 0.6 %slice_bitcast_fusion = f32[2,2,128]{2,1,0:T(2,128)} fusion(f32[4,2,2,128]{3,2,1,0:T(2,128)S(1)} %shard_map.104), kind=kLoop, calls=%fused_computation | loop fusion | bytes 4096 | tf_op jit(solution)/shard_map/squeeze | solution.py:432
  26.0 0.6 %slice.7 = f32[3,2,2,128]{3,2,1,0:T(2,128)} slice(f32[4,2,2,128]{3,2,1,0:T(2,128)S(1)} %shard_map.104), slice={[0:3], [0:2], [0:2], [0:128]} | slice | bytes 12288 | tf_op jit(solution)/shard_map/slice | solution.py:432

commit v4 on v3

--- a/solution.py
+++ b/solution.py
@@ -139,6 +139,17 @@
         axis=1)
     out_col = jnp.broadcast_to(out_ref[...], (n, lat)).T
 
+    cells = [(a, b) for a in range(bz - 1, 2 * bz + 1) for b in range(bx - 1, 2 * bx + 1)]
+    row_n = lax.broadcasted_iota(jnp.int32, (n, n), 0)
+
+    def hots_of(i, part):
+        o = part[5:6].astype(jnp.int32)
+        ct[i] = (row_n == part[4:5].astype(jnp.int32)).astype(F32).astype(BF16)
+        ot[i] = (row_n == (o & 127)).astype(F32).astype(BF16)
+
+    mine = [i for i, (a, b) in enumerate(cells) if bz <= a < 2 * bz and bx <= b < 2 * bx]
+    for i in mine:
+        hots_of(i, own[cells[i][0] - bz, cells[i][1] - bx])
     for copy in first:
         copy.wait()
 
@@ -157,20 +168,16 @@
             hi = rounded(part)
             tab[a, b] = jnp.concatenate([hi, part - hi], axis=0).astype(BF16)
 
-    cells = [(a, b) for a in range(bz - 1, 2 * bz + 1) for b in range(bx - 1, 2 * bx + 1)]
     cx = bx + 2
     total = len(cells)
-    row_n = lax.broadcasted_iota(jnp.int32, (n, n), 0)
     row_s = lax.broadcasted_iota(jnp.int32, (spec, n), 0).astype(F32)
     for i, (a, b) in enumerate(cells):
         part = block(a, b)
-        c = part[4:5].astype(jnp.int32)
         o = part[5:6].astype(jnp.int32)
         p = o >> 7
-        hot_c = (row_n == c).astype(F32).astype(BF16)
-        hot_o = (row_n == (o & 127)).astype(F32).astype(BF16)
-        ct[i] = hot_c
-        ot[i] = hot_o
+        if i not in mine:
+            hots_of(i, part)
+        hot_c, hot_o = ct[i], ot[i]
         at_c = dot(tab[a, b], hot_c)
         at_c = at_c[:8] + at_c[8:]
         around = jnp.concatenate(
@@ -215,7 +222,7 @@
         if bz <= a < 2 * bz and bx <= b < 2 * bx:
             interior[i] = (a - bz) * bx + (b - bx)
 
-    group = 2 if total % 2 == 0 else 1
+    group = 4 if total % 4 == 0 else 1
     for g in range(0, total, group):
         ids = list(range(g, g + group))
         span = slice(g * n, (g + group) * n)
@@ -347,7 +354,25 @@
         gr[:, m + 4, :] = d_m - hi
 
     grad[...] = jnp.zeros_like(grad)
-    for i, (a, b) in enumerate(cells):
+    second = {}
+
+    def give(ready):
+        for key, s in others_list:
+            if s in second or not ready(s):
+                continue
+            t = mirror(key)
+            second[s] = pltpu.make_async_remote_copy(
+                src_ref=grad.at[s], dst_ref=back.at[t - 1], send_sem=send2.at[s - 1],
+                recv_sem=recv2.at[t - 1], device_id=device(key), device_id_type=MESH,
+            )
+            second[s].start()
+
+    order = sorted(range(total), key=lambda i: (-cells[i][0], cells[i][1]))
+    targets = [
+        {place(cells[i][0] + dz, cells[i][1] + dx)[0] for dz in (-1, 0, 1) for dx in (-1, 0, 1)}
+        for i in order]
+    for turn, i in enumerate(order):
+        a, b = cells[i]
         g8 = gr[i]
         p = rows_p[i : i + 1]
         at_c = dot_t(jnp.concatenate([g8, jnp.zeros_like(g8)], axis=0).astype(BF16), ct[i])
@@ -358,17 +383,11 @@
         for off in range(9):
             s, y, x = place(a + off // 3 - 1, b + off % 3 - 1)
             grad[s, y, x] += at_o[8 * off : 8 * off + 8]
-
-    second = []
-    for key, s in others_list:
-        t = mirror(key)
-        copy = pltpu.make_async_remote_copy(
-            src_ref=grad.at[s], dst_ref=back.at[t - 1], send_sem=send2.at[s - 1],
-            recv_sem=recv2.at[t - 1], device_id=device(key), device_id_type=MESH,
-        )
-        copy.start()
-        second.append(copy)
-    for copy in second:
+        if turn + 1 < total and b == cells[-1][1]:
+            later = set().union(*targets[turn + 1 :])
+            give(lambda s: s not in later)
+    give(lambda s: True)
+    for copy in second.values():
         copy.wait()
     for a in range(bz):
         for b in range(bx):

time: 26.7 us -> 24.5 us (0.918)
  Pallas kernels: 24.7 us -> 22.4 us
    pallas_call x1, Pallas kernels: 24.7 us -> 22.4 us  [body(): pl.pallas_call(functools.partial(kernel, nz, nx, bz, bx, nb, spec, ch, la...]
where the time goes in v4:
time: 24.5 us; the launch traced here: 24.3 us
  Pallas kernels  22.4 us (91%)
  local copies, waits for them, and re-layouts  1.17 us (5%)
  between operations  0.64 us (3%)
    pallas_call x1, Pallas kernels, body(): pl.pallas_call(functools.partial(kernel, nz, nx, bz, bx, nb, spec, ch, la...  22.4 us
    slice x1, local copies, waits for them, and re-layouts, body(): return (result[3], result[:3])  0.59 us
    squeeze x1, local copies, waits for them, and re-layouts, body(): return (result[3], result[:3])  0.58 us

profile of v4, /device:TPU:0, one launch (start us, length us, event | category | flops | bytes accessed | tf_op | source)
XLA Modules:
  0.0 24.3 jit_solution(13469473088916171576)
XLA Ops:
  0.6 22.4 %shard_map.104 = f32[4,2,2,128]{3,2,1,0:T(2,128)S(1)} custom-call(f32[3,2,2,128]{3,2,1,0:T(2,128)} %coords_hbm.1, s32[2,2,128]{2,1,0:T(2,128)} %species_hbm.1, s32[2,2,128]{2,1,0:T(2,128)} %centers_hbm.1, s32[2,2,128]{2,1,0:T(2,128)} %others_hbm.1, s32[2,2]{1,0:T(2,128)} %live_hbm.1, f32[24,128]{1,0:T(8,128)} %in_hbm.1, f32[32,128]{1,0:T(8,128)} %bitcast.4, ...), custom_call_target="tpu_custom_call" | custom-call | tf_op jit(solution)/shard_map/pallas_call | solution.py:443
  23.1 0.6 %slice_bitcast_fusion = f32[2,2,128]{2,1,0:T(2,128)} fusion(f32[4,2,2,128]{3,2,1,0:T(2,128)S(1)} %shard_map.104), kind=kLoop, calls=%fused_computation | loop fusion | bytes 4096 | tf_op jit(solution)/shard_map/squeeze | solution.py:451
  23.7 0.6 %slice.7 = f32[3,2,2,128]{3,2,1,0:T(2,128)} slice(f32[4,2,2,128]{3,2,1,0:T(2,128)S(1)} %shard_map.104), slice={[0:3], [0:2], [0:2], [0:128]} | slice | bytes 12288 | tf_op jit(solution)/shard_map/slice | solution.py:451
